TPU v7x, 256 devices: a whole 4x4x8 slice. The times are simulated.
256 devices in a mesh: expert: 64 (over x, z, core), mp: 4 (over y).
Axes of the slice: x: 4, y: 4, z: 8, core: 2. Of those that a mesh axis runs over, the one named last changes fastest.
Arguments:
- tokens: bfloat16 [1536, 6144], P('expert', 'mp'), may hold values from -6 to 6
- mix_weights: float32 [1536, 2], P('expert'), may hold values from 0.2 to 1
- routes: int32 [1536, 2], P('expert'), may hold values from 0 to 7, as said below
- w_gate: bfloat16 [64, 6144, 1024], P('expert', None, 'mp'), may hold values from -0.078125 to 0.078125
- w_up: bfloat16 [64, 6144, 1024], P('expert', None, 'mp'), may hold values from -0.078125 to 0.078125
- w_down: bfloat16 [64, 1024, 6144], P('expert', 'mp'), may hold values from -0.0625 to 0.0625
Outputs:
- mixed_out: bfloat16 [1536, 6144], P('expert', 'mp')
Inputs may be any that keep to these rules, and one draw needn't show every extreme that they name: `routes`: each row names 2 different experts, and every expert is named by some row. Among the 24 rows of one index of the expert axis no expert is named more than 12 times, and on some indices one is named exactly 12 times.
All inputs are finite; a program needn't handle non-finite values.
Results may differ from a plain program's by a relative error of at most 0.011.
Values may be sent and summed in bfloat16 or wider, within the bound.
No kernel may reach another device: no remote copies, remote signals or barrier semaphores. Data moves between devices by JAX's collectives and lax.ppermute only.
A program may use at most 128 MiB of HBM per device.

v0:
```python
import jax
import jax.numpy as jnp
from jax import lax
from jax.sharding import Mesh
from jax.sharding import PartitionSpec as P

EXPERTS = 8
TOP = 2
EXPERT = ("expert_0", "expert_1", "expert_2")


def joined_along(pieces, dim):
    shape = list(pieces.shape[1:])
    shape[dim] *= pieces.shape[0]
    return jnp.moveaxis(pieces, 0, dim).reshape(shape)


def copy_for_each(value, axis):
    size = lax.axis_size(axis)
    return lax.all_to_all(
        jnp.broadcast_to(value[None], (size, *value.shape)), axis, 0, 0, tiled=True
    )


def collect(value, axis, dim):
    return joined_along(copy_for_each(value, axis), dim)


def split_up(value, dim, size):
    shape = value.shape
    pieces = value.reshape(*shape[:dim], size, shape[dim] // size, *shape[dim + 1 :])
    return jnp.moveaxis(pieces, dim, 0)


def exchange_in_order(pieces, axes, sequence):
    shape = [lax.axis_size(a) for a in axes]
    pieces = pieces.reshape(*shape, *pieces.shape[1:])
    for k in sequence:
        pieces = lax.all_to_all(pieces, axes[k], split_axis=k, concat_axis=k, tiled=True)
    return pieces.reshape(-1, *pieces.shape[len(axes) :])


def exchange_by_chip(value, groups, sequence, split_dim, concat_dim):
    size = lax.axis_size(groups[0]) * lax.axis_size(groups[1])
    pieces = split_up(value, split_dim, size)
    return joined_along(exchange_in_order(pieces, groups, sequence), concat_dim)


def pack_rows(pick_tokens, features, repeats):
    packed = jnp.einsum(
        "tem,tc->emc", pick_tokens, features, preferred_element_type=jnp.float32
    ).astype(jnp.bfloat16)
    spread = jnp.broadcast_to(packed[:, None], (packed.shape[0], repeats) + packed.shape[1:])
    return spread.reshape((packed.shape[0] * repeats,) + packed.shape[1:])


def activate(gate_act, up_act):
    return (jax.nn.silu(gate_act) * up_act).astype(jnp.bfloat16)


def local(tokens, mix_weights, routes, w_gate, w_up, w_down):
    tok_rows = tokens.shape[0]
    senders = lax.axis_size(EXPERT)
    group_size = senders // EXPERTS
    capacity = 5 * tok_rows * senders * TOP // (4 * EXPERTS)
    most_rows = tok_rows // 2
    labels = jnp.arange(EXPERTS, dtype=jnp.int32)
    flat_ids = routes.reshape(-1)
    marked = (flat_ids[:, None] == labels[None, :]).astype(jnp.int32)
    earlier = jnp.cumsum(marked, axis=0) - marked
    local_rank = jnp.sum(earlier * marked, axis=1)
    counts = jnp.sum(marked, axis=0)
    count_grid = collect(counts[None, :], EXPERT, 0)
    my_index = lax.axis_index(EXPERT)
    sender_ids = jnp.arange(senders, dtype=jnp.int32)
    lower_mask = (sender_ids[:, None] < my_index).astype(jnp.int32)
    offsets = jnp.sum(count_grid * lower_mask, axis=0)
    slot_ids = jnp.sum(marked * offsets[None, :], axis=1) + local_rank
    keep_mask = (slot_ids < capacity).astype(jnp.int32)
    rank_hit = (local_rank[:, None] == jnp.arange(most_rows, dtype=jnp.int32)[None, :]).astype(
        jnp.int32
    ) * keep_mask[:, None]
    assign_pick = marked[:, :, None] * rank_hit[:, None, :]
    pick_tokens = jnp.sum(assign_pick.reshape(tok_rows, TOP, EXPERTS, most_rows), axis=1).astype(
        jnp.bfloat16
    )
    weighted = assign_pick.astype(jnp.float32) * mix_weights.reshape(-1)[:, None, None]
    combine_w = jnp.sum(weighted.reshape(tok_rows, TOP, EXPERTS * most_rows), axis=1)
    gate_rows = w_gate[0]
    up_rows = w_up[0]
    down_rows = w_down[0]
    arrived = lax.all_to_all(
        pack_rows(pick_tokens, tokens, group_size), EXPERT, split_axis=0, concat_axis=0, tiled=True
    )
    arrived_rows = arrived.reshape(senders * most_rows, arrived.shape[2])
    my_expert = my_index // group_size
    column_counts = jnp.sum(count_grid * (labels[None, :] == my_expert).astype(jnp.int32), axis=1)
    starts = jnp.cumsum(column_counts) - column_counts
    slot_pos = jnp.arange(capacity, dtype=jnp.int32)
    slot_ends = starts + column_counts
    source_of = jnp.minimum(
        jnp.sum((slot_ends[None, :] <= slot_pos[:, None]).astype(jnp.int32), axis=1), senders - 1
    )
    source_hit = (sender_ids[None, :] == source_of[:, None]).astype(jnp.int32)
    start_of = jnp.sum(source_hit * starts[None, :], axis=1)
    slot_valid = slot_pos < jnp.sum(column_counts)
    fetch_idx = jnp.where(slot_valid, source_of * most_rows + slot_pos - start_of, 0)
    in_rows = jnp.where(
        slot_valid[:, None], jnp.take(arrived_rows, fetch_idx, axis=0), jnp.zeros((), jnp.bfloat16)
    )
    shard_piece = lax.all_gather(in_rows, "mp", axis=1, tiled=True)
    gate_act = jnp.dot(shard_piece, gate_rows, preferred_element_type=jnp.float32)
    up_act = jnp.dot(shard_piece, up_rows, preferred_element_type=jnp.float32)
    hidden = activate(gate_act, up_act)
    part_sum = jnp.dot(hidden, down_rows, preferred_element_type=jnp.float32)
    reduced = lax.psum_scatter(part_sum.astype(jnp.bfloat16), "mp", scatter_dimension=1, tiled=True)
    out_width = reduced.shape[1]
    buffer_pos = jnp.arange(most_rows, dtype=jnp.int32)
    slot_back = starts[:, None] + buffer_pos[None, :]
    back_valid = (buffer_pos[None, :] < column_counts[:, None]) & (slot_back < capacity)
    back_idx = jnp.where(back_valid, slot_back, 0).reshape(-1)
    back_rows = jnp.where(
        back_valid.reshape(-1)[:, None],
        jnp.take(reduced, back_idx, axis=0),
        jnp.zeros((), jnp.bfloat16),
    )
    returned = exchange_by_chip(
        back_rows.reshape(senders, most_rows, out_width),
        (("expert_0", "expert_1"), "expert_2"),
        (1, 0),
        0,
        0,
    )
    summed = jnp.sum(
        returned.reshape(EXPERTS, group_size, most_rows, out_width).astype(jnp.float32), axis=1
    )
    result = jnp.dot(
        combine_w, summed.reshape(EXPERTS * most_rows, out_width), precision=lax.Precision.HIGHEST
    )
    return result.astype(jnp.bfloat16)


def solution(mesh):
    torus = Mesh(
        mesh.devices.reshape(4, 8, 2, mesh.shape["mp"]), ("expert_0", "expert_1", "expert_2", "mp")
    )
    placed = (
        P(EXPERT, "mp"),
        P(EXPERT, None),
        P(EXPERT, None),
        P(EXPERT, None, "mp"),
        P(EXPERT, None, "mp"),
        P(EXPERT, "mp", None),
    )
    return jax.shard_map(
        local, mesh=torus, in_specs=placed, out_specs=P(EXPERT, "mp"), check_vma=False
    )
```

profile of v0, /device:TPU:6, one launch (start us, length us, event | category | flops | bytes accessed | tf_op | source)
XLA Modules:
  0.0 377.2 jit_solution(595688700204690243)
XLA Ops:
  6.5 0.9 copy.54
  7.4 0.1 eq.76
  7.6 0.6 broadcast_in_dim.86
  8.3 12.2 %all-to-all-start = ((s32[64,1,8]{2,1,0:T(1,128)}), s32[64,1,8]{2,1,0:T(1,128)S(1)}, u32[]{:S(2)}, u32[]{:S(2)}) async-start(s32[64,1,8]{2,1,0:T(1,128)} %broadcast_in_dim.86), calls=%async_computation | async-start | bytes 65536 | tf_op jit(solution)/shard_map/all_to_all | solution.py:20
  20.5 0.7 fusion.18
  21.3 6.7 %all-to-all-done = s32[64,1,8]{2,1,0:T(1,128)S(1)} async-done(((s32[64,1,8]{2,1,0:T(1,128)}), s32[64,1,8]{2,1,0:T(1,128)S(1)}, u32[]{:S(2)}, u32[]{:S(2)}) %all-to-all-start) | async-done | bytes 2080 | tf_op jit(solution)/shard_map/all_to_all | solution.py:20
  28.0 0.7 fusion.20
  28.8 0.2 select_reduce_fusion.2
  29.4 1.1 convolution_convert_fusion.1
  30.5 2.1 broadcast_in_dim.93
  32.6 7.5 %all-to-all-start.1 = ((bf16[64,12,1536]{2,1,0:T(8,128)(2,1)}), bf16[64,12,1536]{2,1,0:T(8,128)(2,1)}, u32[]{:S(2)}, u32[]{:S(2)}) async-start(bf16[64,12,1536]{2,1,0:T(8,128)(2,1)} %bitcast.37), calls=%async_computation.1 | async-start | bytes 6291456 | tf_op jit(solution)/shard_map/all_to_all | solution.py:92
  40.1 0.1 copy.57
  40.2 0.1 reduce-window.4
  40.3 0.1 reduce.3
  40.4 0.1 convert_reduce_fusion.1
  40.5 0.1 select_reduce_fusion
  40.6 0.7 compare_select_fusion.2
  41.3 0.7 iota_compare_fusion.7
  41.9 68.9 %all-to-all-done.1 = bf16[64,12,1536]{2,1,0:T(8,128)(2,1)} async-done(((bf16[64,12,1536]{2,1,0:T(8,128)(2,1)}), bf16[64,12,1536]{2,1,0:T(8,128)(2,1)}, u32[]{:S(2)}, u32[]{:S(2)}) %all-to-all-start.1) | async-done | bytes 2359328 | tf_op jit(solution)/shard_map/all_to_all | solution.py:92
  110.9 4.9 %reshape.343 = bf16[768,1536]{1,0:T(8,128)(2,1)} reshape(bf16[64,12,1536]{2,1,0:T(8,128)(2,1)} %all-to-all-done.1) | data formatting | bytes 4718592 | tf_op jit(solution)/shard_map/reshape | solution.py:95
  115.8 6.4 %gather_fusion = bf16[480,1536]{1,0:T(8,128)(2,1)} fusion(bf16[768,1536]{1,0:T(8,128)(2,1)} %reshape.343, s32[1024]{0:T(1024)S(1)} %pad_clamp_fusion.1), kind=kCustom, calls=%fused_computation | custom fusion | bytes 2951040 | tf_op jit(solution)/shard_map/jit(_take)/gather | solution.py:109
  122.1 2.8 select_select_fusion.1
  124.9 0.2 reduce-scatter.2.cloned.1.call-start
  125.1 63.9 %all-gather.2.cloned.1.call-done = bf16[480,6144]{1,0:T(8,128)(2,1)} async-done(((bf16[480,1536]{1,0:T(8,128)(2,1)}), bf16[480,6144]{1,0:T(8,128)(2,1)}) %all-gather.2.cloned.1.call-update) | async-done | bytes 5898256 | tf_op jit(solution)/shard_map/all_gather | solution.py:111
  189.1 5.4 %fusion.3 = f32[480,256]{1,0:T(8,128)S(1)} fusion(bf16[480,6144]{1,0:T(8,128)(2,1)} %all-gather.2.cloned.1.call-done, bf16[1,6144,256]{2,1,0:T(8,128)(2,1)} %param.9), kind=kOutput, calls=%fused_computation.8 | convolution fusion | flops 1509949440 | bytes 9535488 | tf_op jit(solution)/shard_map/dot_general | solution.py:112
  194.5 0.8 copy-done.3
  195.3 1.7 fusion.8
  197.0 4.2 %convolution_convert_fusion = bf16[480,6144]{1,0:T(8,128)(2,1)} fusion(bf16[480,256]{1,0:T(8,128)(2,1)S(1)} %fusion.8, bf16[1,256,6144]{2,1,0:T(8,128)(2,1)S(1)} %copy-done), kind=kOutput, calls=%fused_computation.2 | convolution fusion | flops 1512898560 | bytes 9289728 | tf_op jit(solution)/shard_map/dot_general | solution.py:115
  201.4 0.1 lt.154
  201.5 0.1 add.125
  201.7 0.1 lt.172
  201.9 0.2 compare_and_fusion.1
  202.1 63.3 %reduce-scatter.2.cloned.1.call-done = bf16[480,1536]{1,0:T(8,128)(2,1)} async-done(((bf16[480,6144]{1,0:T(8,128)(2,1)}), bf16[480,1536]{1,0:T(8,128)(2,1)}) %reduce-scatter.2.cloned.1.call-update) | async-done | bytes 1474576 | tf_op jit(solution)/shard_map/reduce_scatter | solution.py:116
  265.4 7.5 %gather_fusion.1 = bf16[768,1536]{1,0:T(8,128)(2,1)} fusion(bf16[480,1536]{1,0:T(8,128)(2,1)} %reduce-scatter.2.cloned.1.call-done, s32[1024]{0:T(1024)S(1)} %pad_clamp_fusion), kind=kCustom, calls=%fused_computation.1 | custom fusion | bytes 4721664 | tf_op jit(solution)/shard_map/jit(_take)/gather | solution.py:124
  272.8 4.8 %gather.12 = bf16[32,2,1,12,1536]{4,3,1,0,2:T(8,128)(2,1)} reshape(bf16[768,1536]{1,0:T(8,128)(2,1)} %gather_fusion.1) | data formatting | bytes 4718592 | tf_op jit(solution)/shard_map/jit(_take)/gather | solution.py:124
  277.6 2.2 select_select_fusion
  279.8 1.3 copy.61
  281.1 5.6 %all_to_all.20 = bf16[32,2,1,12,1536]{4,0,3,2,1:T(8,128)(2,1)S(1)} all-to-all(bf16[32,2,1,12,1536]{4,0,3,2,1:T(8,128)(2,1)S(1)} %copy.61), channel_id=1, replica_groups=mesh['expert_0'=4,'expert_1'=8,'expert_2'=2,'mp'=4] {'expert_2'}, dimensions={1} | all-to-all | bytes 4718592 | tf_op jit(solution)/shard_map/all_to_all | solution.py:39
  286.7 3.8 %copy.62 = bf16[32,2,1,12,1536]{4,1,3,2,0:T(2,128)(2,1)} copy(bf16[32,2,1,12,1536]{4,0,3,2,1:T(8,128)(2,1)S(1)} %all_to_all.20) | data formatting | bytes 4718592 | tf_op jit(solution)/shard_map/all_to_all | solution.py:39
  290.5 10.4 %all-to-all-start.3 = ((bf16[32,2,1,12,1536]{4,1,3,2,0:T(2,128)(2,1)}), bf16[32,2,1,12,1536]{4,1,3,2,0:T(2,128)(2,1)}, u32[]{:S(2)}, u32[]{:S(2)}) async-start(bf16[32,2,1,12,1536]{4,1,3,2,0:T(2,128)(2,1)} %copy.62), calls=%async_computation.4 | async-start | bytes 4718592 | tf_op jit(solution)/shard_map/all_to_all | solution.py:39
  301.1 0.1 multiply_convert_fusion
  301.2 0.1 convert_element_type.71
  301.3 0.1 multiply_reduce_fusion.1
  301.4 55.5 %all-to-all-done.3 = bf16[32,2,1,12,1536]{4,1,3,2,0:T(2,128)(2,1)} async-done(((bf16[32,2,1,12,1536]{4,1,3,2,0:T(2,128)(2,1)}), bf16[32,2,1,12,1536]{4,1,3,2,0:T(2,128)(2,1)}, u32[]{:S(2)}, u32[]{:S(2)}) %all-to-all-start.3) | async-done | bytes 2359328 | tf_op jit(solution)/shard_map/all_to_all | solution.py:39
  356.9 8.2 %convert_reduce_fusion = f32[32,12,1536]{2,1,0:T(8,128)S(1)} fusion(bf16[32,2,1,12,1536]{4,1,3,2,0:T(2,128)(2,1)} %all-to-all-done.3), kind=kLoop, calls=%fused_computation.3 | loop fusion | flops 1769472 | bytes 4718592 | tf_op jit(solution)/shard_map/reduce_sum | solution.py:134
  365.1 1.1 bitcast_reduce_fusion
  366.3 2.0 reshape.344
  368.3 2.1 convolution_convert_fusion.2
  (36 shorter events, 1.2 us)
Async XLA Ops:
  6.5 190.5 %copy-start = (bf16[1,256,6144]{2,1,0:T(8,128)(2,1)S(1)}, bf16[1,256,6144]{2,1,0:T(8,128)(2,1)}, u32[]{:S(2)}) copy-start(bf16[1,256,6144]{2,1,0:T(8,128)(2,1)} %param.11) | copy-start | bytes 9437188
  8.3 19.7 %all-to-all-start = ((s32[64,1,8]{2,1,0:T(1,128)}), s32[64,1,8]{2,1,0:T(1,128)S(1)}, u32[]{:S(2)}, u32[]{:S(2)}) async-start(s32[64,1,8]{2,1,0:T(1,128)} %broadcast_in_dim.86), calls=%async_computation | async-start | bytes 65536 | tf_op jit(solution)/shard_map/all_to_all | solution.py:20
  32.6 78.3 %all-to-all-start.1 = ((bf16[64,12,1536]{2,1,0:T(8,128)(2,1)}), bf16[64,12,1536]{2,1,0:T(8,128)(2,1)}, u32[]{:S(2)}, u32[]{:S(2)}) async-start(bf16[64,12,1536]{2,1,0:T(8,128)(2,1)} %bitcast.37), calls=%async_computation.1 | async-start | bytes 6291456 | tf_op jit(solution)/shard_map/all_to_all | solution.py:92
  40.0 149.1 %all-gather.2.cloned.1.call-start = ((), (), s32[]{:S(2)}) async-start(), calls=%async_computation.5 | async-start | bytes 7372800 | tf_op jit(solution)/shard_map/all_gather | solution.py:111
  124.9 140.4 %reduce-scatter.2.cloned.1.call-start = ((), (), s32[]{:S(2)}) async-start(), calls=%async_computation.6 | async-start | bytes 7372800 | tf_op jit(solution)/shard_map/reduce_scatter | solution.py:116
  189.1 5.5 %copy-start.2 = (bf16[480,6144]{1,0:T(8,128)(2,1)S(1)}, bf16[480,6144]{1,0:T(8,128)(2,1)}, u32[]{:S(2)}) copy-start(bf16[480,6144]{1,0:T(8,128)(2,1)} %all-gather.2.cloned.1.call-done) | copy-start | bytes 17694724
  189.1 6.2 %copy-start.3 = (bf16[1,6144,256]{2,1,0:T(8,128)(2,1)S(1)}, bf16[1,6144,256]{2,1,0:T(8,128)(2,1)}, u32[]{:S(2)}) copy-start(bf16[1,6144,256]{2,1,0:T(8,128)(2,1)} %param.10) | copy-start | bytes 9437188
  290.5 10.4 %copy-start.1 = (f32[24,2]{0,1:T(2,128)S(1)}, f32[24,2]{0,1:T(2,128)}, u32[]{:S(2)}) copy-start(f32[24,2]{0,1:T(2,128)} %param.7) | copy-start | bytes 580
  290.5 66.4 %all-to-all-start.3 = ((bf16[32,2,1,12,1536]{4,1,3,2,0:T(2,128)(2,1)}), bf16[32,2,1,12,1536]{4,1,3,2,0:T(2,128)(2,1)}, u32[]{:S(2)}, u32[]{:S(2)}) async-start(bf16[32,2,1,12,1536]{4,1,3,2,0:T(2,128)(2,1)} %copy.62), calls=%async_computation.4 | async-start | bytes 4718592 | tf_op jit(solution)/shard_map/all_to_all | solution.py:39
Sparse Core Ops, SparseCore 0:
  125.0 63.9 all-gather.1
  201.4 63.9 reduce-scatter.1
where the time goes:
time: 378 us; the launch traced here: 377 us
  waiting for transfers between devices  258 us (68%)
  local copies, waits for them, and re-layouts  36.2 us (10%)
  starting transfers between devices  30.2 us (8%)
  other arithmetic  18.5 us (5%)
  matrix products  14.6 us (4%)
  between operations  13.7 us (4%)
  blocking collectives  5.63 us (1%)
    all_to_all x1, waiting for transfers between devices, local(): lax.all_to_all(pack_rows(pick_tokens, tokens, group_size), EXPERT, split_...  68.9 us
    all_gather x1, waiting for transfers between devices, local(): shard_piece = lax.all_gather(in_rows, 'mp', axis=1, tiled=True)  63.9 us
    reduce_scatter x1, waiting for transfers between devices, local(): lax.psum_scatter(part_sum.astype(jnp.bfloat16), 'mp', scatter_dimension=1...  63.3 us
    all_to_all x1, waiting for transfers between devices, exchange_in_order(): lax.all_to_all(pieces, axes[k], split_axis=k, concat_axis=k, tiled=True)  55.5 us
    gather x2, local copies, waits for them, and re-layouts, local(): jnp.take(reduced, back_idx, axis=0)  12.2 us
    all_to_all x1, starting transfers between devices, copy_for_each(): lax.all_to_all(jnp.broadcast_to(value[None], (size, *value.shape)), axis,...  12.2 us
    all_to_all x1, starting transfers between devices, exchange_in_order(): lax.all_to_all(pieces, axes[k], split_axis=k, concat_axis=k, tiled=True)  10.4 us
    reduce_sum x2, other arithmetic, local(): jnp.sum(returned.reshape(EXPERTS, group_size, most_rows, out_width).astyp...  9.32 us
  transfers between devices with their start and end apart: 5, of which 5 were waited for; matrix products, arithmetic and copies ran while one was open for 1% of the time, Pallas kernels for 0%

commit v1 on v0

--- a/solution.py
+++ b/solution.py
@@ -108,7 +108,21 @@
     in_rows = jnp.where(
         slot_valid[:, None], jnp.take(arrived_rows, fetch_idx, axis=0), jnp.zeros((), jnp.bfloat16)
     )
-    shard_piece = lax.all_gather(in_rows, "mp", axis=1, tiled=True)
+    ways, here, step = (lax.axis_size("mp"), lax.axis_index("mp"), in_rows.shape[1])
+    shape_2 = [n * ways if d == 1 else n for d, n in enumerate(in_rows.shape)]
+    full = lax.dynamic_update_slice_in_dim(
+        jnp.zeros(shape_2, in_rows.dtype), in_rows, here * step, axis=1
+    )
+    going_up = going_down = in_rows
+    for far in range(1, ways // 2 + 1):
+        going_up = lax.ppermute(going_up, "mp", [(d, (d + 1) % ways) for d in range(ways)])
+        full = lax.dynamic_update_slice_in_dim(full, going_up, (here - far) % ways * step, axis=1)
+        if 2 * far < ways:
+            going_down = lax.ppermute(going_down, "mp", [(d, (d - 1) % ways) for d in range(ways)])
+            full = lax.dynamic_update_slice_in_dim(
+                full, going_down, (here + far) % ways * step, axis=1
+            )
+    shard_piece = full
     gate_act = jnp.dot(shard_piece, gate_rows, preferred_element_type=jnp.float32)
     up_act = jnp.dot(shard_piece, up_rows, preferred_element_type=jnp.float32)
     hidden = activate(gate_act, up_act)

time: 378 us -> 386 us (1.021)
  local copies, waits for them, and re-layouts: 36.2 us -> 48.1 us
  waiting for transfers between devices: 258 us -> 253 us
    all_gather x1 -> x0, waiting for transfers between devices: 63.9 us -> none  [local(): shard_piece = lax.all_gather(in_rows, 'mp', axis=1, tiled=True)]
    ppermute x0 -> x3, waiting for transfers between devices: none -> 62.2 us  [the longest x2 62.1 us: local(): lax.ppermute(going_up, 'mp', [(d, (d + 1) % ways) for d in range(ways)])]
    dynamic_update_slice x0 -> x3, local copies, waits for them, and re-layouts: none -> 8.06 us  [the longest x2 5.25 us: local(): lax.dynamic_update_slice_in_dim(full, going_up, (here - far) % ways * ste...]
  transfers between devices with their start and end apart: 5 -> 7, of which waited for: 5 -> 6; matrix products, arithmetic and copies ran while one was open for 1% -> 2% of each run, Pallas kernels for 0% -> 0%
where the time goes in v1:
time: 386 us; the launch traced here: 385 us
  waiting for transfers between devices  253 us (66%)
  local copies, waits for them, and re-layouts  48.1 us (12%)
  starting transfers between devices  33.7 us (9%)
  other arithmetic  17.3 us (4%)
  matrix products  13.7 us (4%)
  between operations  13.7 us (4%)
  blocking collectives  5.63 us (1%)
    all_to_all x1, waiting for transfers between devices, local(): lax.all_to_all(pack_rows(pick_tokens, tokens, group_size), EXPERT, split_...  68.9 us
    ppermute x2, waiting for transfers between devices, local(): lax.ppermute(going_up, 'mp', [(d, (d + 1) % ways) for d in range(ways)])  62.1 us
    reduce_scatter x1, waiting for transfers between devices, local(): lax.psum_scatter(part_sum.astype(jnp.bfloat16), 'mp', scatter_dimension=1...  59.5 us
    all_to_all x1, waiting for transfers between devices, exchange_in_order(): lax.all_to_all(pieces, axes[k], split_axis=k, concat_axis=k, tiled=True)  55.5 us
    gather x2, local copies, waits for them, and re-layouts, local(): jnp.take(reduced, back_idx, axis=0)  12.2 us
    all_to_all x1, starting transfers between devices, copy_for_each(): lax.all_to_all(jnp.broadcast_to(value[None], (size, *value.shape)), axis,...  12.2 us
    all_to_all x1, starting transfers between devices, exchange_in_order(): lax.all_to_all(pieces, axes[k], split_axis=k, concat_axis=k, tiled=True)  10.3 us
    reduce_sum x2, other arithmetic, local(): jnp.sum(returned.reshape(EXPERTS, group_size, most_rows, out_width).astyp...  9.32 us
  transfers between devices with their start and end apart: 7, of which 6 were waited for; matrix products, arithmetic and copies ran while one was open for 2% of the time, Pallas kernels for 0%

profile of v1, /device:TPU:6, one launch (start us, length us, event | category | flops | bytes accessed | tf_op | source)
XLA Modules:
  0.0 384.9 jit_solution(6624097068224139420)
XLA Ops:
  6.5 0.9 copy.54
  7.6 0.6 broadcast_in_dim.89
  8.3 12.2 %all-to-all-start = ((s32[64,1,8]{2,1,0:T(1,128)}), s32[64,1,8]{2,1,0:T(1,128)S(1)}, u32[]{:S(2)}, u32[]{:S(2)}) async-start(s32[64,1,8]{2,1,0:T(1,128)} %broadcast_in_dim.89), calls=%async_computation | async-start | bytes 65536 | tf_op jit(solution)/shard_map/all_to_all | solution.py:20
  20.5 0.7 fusion.13
  21.3 6.7 %all-to-all-done = s32[64,1,8]{2,1,0:T(1,128)S(1)} async-done(((s32[64,1,8]{2,1,0:T(1,128)}), s32[64,1,8]{2,1,0:T(1,128)S(1)}, u32[]{:S(2)}, u32[]{:S(2)}) %all-to-all-start) | async-done | bytes 2080 | tf_op jit(solution)/shard_map/all_to_all | solution.py:20
  28.0 0.7 fusion.15
  28.8 0.2 select_reduce_fusion.2
  29.4 1.1 convolution_convert_fusion.1
  30.5 2.1 broadcast_in_dim.97
  32.6 7.5 %all-to-all-start.1 = ((bf16[64,12,1536]{2,1,0:T(8,128)(2,1)}), bf16[64,12,1536]{2,1,0:T(8,128)(2,1)}, u32[]{:S(2)}, u32[]{:S(2)}) async-start(bf16[64,12,1536]{2,1,0:T(8,128)(2,1)} %bitcast.32), calls=%async_computation.1 | async-start | bytes 6291456 | tf_op jit(solution)/shard_map/all_to_all | solution.py:92
  40.6 0.7 compare_select_fusion.2
  41.3 0.7 iota_compare_fusion.7
  41.9 68.9 %all-to-all-done.1 = bf16[64,12,1536]{2,1,0:T(8,128)(2,1)} async-done(((bf16[64,12,1536]{2,1,0:T(8,128)(2,1)}), bf16[64,12,1536]{2,1,0:T(8,128)(2,1)}, u32[]{:S(2)}, u32[]{:S(2)}) %all-to-all-start.1) | async-done | bytes 2359328 | tf_op jit(solution)/shard_map/all_to_all | solution.py:92
  110.9 4.9 %reshape.343 = bf16[768,1536]{1,0:T(8,128)(2,1)} reshape(bf16[64,12,1536]{2,1,0:T(8,128)(2,1)} %all-to-all-done.1) | data formatting | bytes 4718592 | tf_op jit(solution)/shard_map/reshape | solution.py:95
  115.8 6.3 %gather_fusion = bf16[480,1536]{1,0:T(8,128)(2,1)} fusion(bf16[768,1536]{1,0:T(8,128)(2,1)} %reshape.343, s32[1024]{0:T(1024)S(1)} %pad_clamp_fusion.1), kind=kCustom, calls=%fused_computation | custom fusion | bytes 2951040 | tf_op jit(solution)/shard_map/jit(_take)/gather | solution.py:109
  122.1 0.7 broadcast_in_dim.93
  122.8 0.7 copy-done.1
  123.5 1.6 constant_dynamic-update-slice_fusion.3
  125.1 2.5 copy-done.2
  127.6 1.6 collective-permute-start
  129.2 1.7 collective-permute-start.1
  130.8 31.8 %collective-permute-done = bf16[480,1536]{1,0:T(8,128)(2,1)} collective-permute-done((bf16[480,1536]{1,0:T(8,128)(2,1)}, bf16[480,1536]{1,0:T(8,128)(2,1)}, u32[]{:S(2)}, u32[]{:S(2)}) %collective-permute-start) | collective-permute-done | bytes 1474592 | tf_op jit(solution)/shard_map/ppermute | solution.py:118
  162.7 0.4 collective-permute-start.2
  163.1 2.6 constant_dynamic-update-slice_fusion.2
  165.7 2.8 constant_dynamic-update-slice_fusion.1
  168.5 30.3 %collective-permute-done.2 = bf16[480,1536]{1,0:T(8,128)(2,1)} collective-permute-done((bf16[480,1536]{1,0:T(8,128)(2,1)}, bf16[480,1536]{1,0:T(8,128)(2,1)}, u32[]{:S(2)}, u32[]{:S(2)}) %collective-permute-start.2) | collective-permute-done | bytes 1474592 | tf_op jit(solution)/shard_map/ppermute | solution.py:118
  198.9 2.6 constant_dynamic-update-slice_fusion
  201.5 4.6 %fusion.1 = f32[480,256]{1,0:T(8,128)S(1)} fusion(bf16[480,6144]{1,0:T(8,128)(2,1)} %constant_dynamic-update-slice_fusion, bf16[1,6144,256]{2,1,0:T(8,128)(2,1)S(1)} %copy-done.5), kind=kOutput, calls=%fused_computation.6 | convolution fusion | flops 1509949440 | bytes 9535488 | tf_op jit(solution)/shard_map/dot_general | solution.py:127
  206.1 0.8 copy-done.6
  206.8 1.7 fusion.3
  208.5 4.3 %convolution_convert_fusion = bf16[480,6144]{1,0:T(8,128)(2,1)} fusion(bf16[1,256,6144]{2,1,0:T(8,128)(2,1)S(1)} %copy-done, f32[480,256]{1,0:T(8,128)S(1)} %fusion.1, f32[480,256]{1,0:T(8,128)S(1)} %fusion.3), kind=kOutput, calls=%fused_computation.2 | convolution fusion | flops 1513635840 | bytes 10027008 | tf_op jit(solution)/shard_map/dot_general | solution.py:129
  213.3 0.1 lt.205
  213.5 0.2 compare_and_fusion.1
  213.6 59.5 %reduce-scatter.2.cloned.1.call-done = bf16[480,1536]{1,0:T(8,128)(2,1)} async-done(((bf16[480,6144]{1,0:T(8,128)(2,1)}), bf16[480,1536]{1,0:T(8,128)(2,1)}) %reduce-scatter.2.cloned.1.call-update) | async-done | bytes 1474576 | tf_op jit(solution)/shard_map/reduce_scatter | solution.py:130
  273.1 7.5 %gather_fusion.1 = bf16[768,1536]{1,0:T(8,128)(2,1)} fusion(bf16[480,1536]{1,0:T(8,128)(2,1)} %reduce-scatter.2.cloned.1.call-done, s32[1024]{0:T(1024)S(1)} %pad_clamp_fusion), kind=kCustom, calls=%fused_computation.1 | custom fusion | bytes 4721664 | tf_op jit(solution)/shard_map/jit(_take)/gather | solution.py:138
  280.5 4.8 %gather.12 = bf16[32,2,1,12,1536]{4,3,1,0,2:T(8,128)(2,1)} reshape(bf16[768,1536]{1,0:T(8,128)(2,1)} %gather_fusion.1) | data formatting | bytes 4718592 | tf_op jit(solution)/shard_map/jit(_take)/gather | solution.py:138
  285.3 2.2 select_select_fusion
  287.5 1.3 copy.61
  288.8 5.6 %all_to_all.20 = bf16[32,2,1,12,1536]{4,0,3,2,1:T(8,128)(2,1)S(1)} all-to-all(bf16[32,2,1,12,1536]{4,0,3,2,1:T(8,128)(2,1)S(1)} %copy.61), channel_id=1, replica_groups=mesh['expert_0'=4,'expert_1'=8,'expert_2'=2,'mp'=4] {'expert_2'}, dimensions={1} | all-to-all | bytes 4718592 | tf_op jit(solution)/shard_map/all_to_all | solution.py:39
  294.4 3.8 copy.62
  298.2 10.3 %all-to-all-start.3 = ((bf16[32,2,1,12,1536]{4,1,3,2,0:T(2,128)(2,1)}), bf16[32,2,1,12,1536]{4,1,3,2,0:T(2,128)(2,1)}, u32[]{:S(2)}, u32[]{:S(2)}) async-start(bf16[32,2,1,12,1536]{4,1,3,2,0:T(2,128)(2,1)} %copy.62), calls=%async_computation.4 | async-start | bytes 4718592 | tf_op jit(solution)/shard_map/all_to_all | solution.py:39
  308.8 0.1 multiply_convert_fusion.2
  308.9 0.1 convert_element_type.71
  309.1 55.5 %all-to-all-done.3 = bf16[32,2,1,12,1536]{4,1,3,2,0:T(2,128)(2,1)} async-done(((bf16[32,2,1,12,1536]{4,1,3,2,0:T(2,128)(2,1)}), bf16[32,2,1,12,1536]{4,1,3,2,0:T(2,128)(2,1)}, u32[]{:S(2)}, u32[]{:S(2)}) %all-to-all-start.3) | async-done | bytes 2359328 | tf_op jit(solution)/shard_map/all_to_all | solution.py:39
  364.6 8.2 %convert_reduce_fusion = f32[32,12,1536]{2,1,0:T(8,128)S(1)} fusion(bf16[32,2,1,12,1536]{4,1,3,2,0:T(2,128)(2,1)} %all-to-all-done.3), kind=kLoop, calls=%fused_computation.3 | loop fusion | flops 1769472 | bytes 4718592 | tf_op jit(solution)/shard_map/reduce_sum | solution.py:148
  372.8 1.1 bitcast_reduce_fusion
  374.0 2.0 reshape.344
  376.0 2.1 convolution_convert_fusion.2
  (49 shorter events, 2.1 us)
Async XLA Ops:
  6.5 202.0 %copy-start = (bf16[1,256,6144]{2,1,0:T(8,128)(2,1)S(1)}, bf16[1,256,6144]{2,1,0:T(8,128)(2,1)}, u32[]{:S(2)}) copy-start(bf16[1,256,6144]{2,1,0:T(8,128)(2,1)} %param.11) | copy-start | bytes 9437188
  8.3 19.7 %all-to-all-start = ((s32[64,1,8]{2,1,0:T(1,128)}), s32[64,1,8]{2,1,0:T(1,128)S(1)}, u32[]{:S(2)}, u32[]{:S(2)}) async-start(s32[64,1,8]{2,1,0:T(1,128)} %broadcast_in_dim.89), calls=%async_computation | async-start | bytes 65536 | tf_op jit(solution)/shard_map/all_to_all | solution.py:20
  32.6 78.3 %all-to-all-start.1 = ((bf16[64,12,1536]{2,1,0:T(8,128)(2,1)}), bf16[64,12,1536]{2,1,0:T(8,128)(2,1)}, u32[]{:S(2)}, u32[]{:S(2)}) async-start(bf16[64,12,1536]{2,1,0:T(8,128)(2,1)} %bitcast.32), calls=%async_computation.1 | async-start | bytes 6291456 | tf_op jit(solution)/shard_map/all_to_all | solution.py:92
  40.0 233.0 %reduce-scatter.2.cloned.1.call-start = ((), (), s32[]{:S(2)}) async-start(), calls=%async_computation.5 | async-start | bytes 7372800 | tf_op jit(solution)/shard_map/reduce_scatter | solution.py:130
  122.1 1.4 copy-start.1
  125.1 2.5 copy-start.2
  127.6 35.0 %collective-permute-start = (bf16[480,1536]{1,0:T(8,128)(2,1)}, bf16[480,1536]{1,0:T(8,128)(2,1)}, u32[]{:S(2)}, u32[]{:S(2)}) collective-permute-start(bf16[480,1536]{1,0:T(8,128)(2,1)} %get-tuple-element.11), channel_id=1, source_target_pairs={{0,1},{1,2},{2,3},{3,0},{4,5},{5,6},{6,7},{7,4},{8,9},{9,10},{10,1... | collective-permute-start | bytes 4423688 | tf_op jit(solution)/shard_map/ppermute | solution.py:118
  129.2 36.5 %collective-permute-start.1 = (bf16[480,1536]{1,0:T(8,128)(2,1)}, bf16[480,1536]{1,0:T(8,128)(2,1)}, u32[]{:S(2)}, u32[]{:S(2)}) collective-permute-start(bf16[480,1536]{1,0:T(8,128)(2,1)} %get-tuple-element.11), channel_id=1, source_target_pairs={{0,3},{1,0},{2,1},{3,2},{4,7},{5,4},{6,5},{7,6},{8,11},{9,8},{10,9... | collective-permute-start | bytes 4423688 | tf_op jit(solution)/shard_map/ppermute | solution.py:121
  162.7 36.2 %collective-permute-start.2 = (bf16[480,1536]{1,0:T(8,128)(2,1)}, bf16[480,1536]{1,0:T(8,128)(2,1)}, u32[]{:S(2)}, u32[]{:S(2)}) collective-permute-start(bf16[480,1536]{1,0:T(8,128)(2,1)} %collective-permute-done), channel_id=1, source_target_pairs={{0,1},{1,2},{2,3},{3,0},{4,5},{5,6},{6,7},{7,4},{8,9},{9,10},{10,1... | collective-permute-start | bytes 4423688 | tf_op jit(solution)/shard_map/ppermute | solution.py:118
  165.7 35.8 %copy-start.5 = (bf16[1,6144,256]{2,1,0:T(8,128)(2,1)S(1)}, bf16[1,6144,256]{2,1,0:T(8,128)(2,1)}, u32[]{:S(2)}) copy-start(bf16[1,6144,256]{2,1,0:T(8,128)(2,1)} %param.10) | copy-start | bytes 9437188
  201.5 4.6 %copy-start.3 = (bf16[480,6144]{1,0:T(8,128)(2,1)S(1)}, bf16[480,6144]{1,0:T(8,128)(2,1)}, u32[]{:S(2)}) copy-start(bf16[480,6144]{1,0:T(8,128)(2,1)} %constant_dynamic-update-slice_fusion) | copy-start | bytes 17694724
  201.5 5.3 %copy-start.6 = (bf16[1,6144,256]{2,1,0:T(8,128)(2,1)S(1)}, bf16[1,6144,256]{2,1,0:T(8,128)(2,1)}, u32[]{:S(2)}) copy-start(bf16[1,6144,256]{2,1,0:T(8,128)(2,1)} %param.9) | copy-start | bytes 9437188
  298.2 10.4 %copy-start.4 = (f32[24,2]{0,1:T(2,128)S(1)}, f32[24,2]{0,1:T(2,128)}, u32[]{:S(2)}) copy-start(f32[24,2]{0,1:T(2,128)} %param.7) | copy-start | bytes 580
  298.2 66.4 %all-to-all-start.3 = ((bf16[32,2,1,12,1536]{4,1,3,2,0:T(2,128)(2,1)}), bf16[32,2,1,12,1536]{4,1,3,2,0:T(2,128)(2,1)}, u32[]{:S(2)}, u32[]{:S(2)}) async-start(bf16[32,2,1,12,1536]{4,1,3,2,0:T(2,128)(2,1)} %copy.62), calls=%async_computation.4 | async-start | bytes 4718592 | tf_op jit(solution)/shard_map/all_to_all | solution.py:39
Sparse Core Ops, SparseCore 0:
  212.9 60.1 reduce-scatter.1
